TPU v7x, 32 devices: a whole 2x2x4 slice. The times are simulated.
32 devices in a mesh: seg: 4 (over z), ch: 8 (over y, x, core).
Axes of the slice: x: 2, y: 2, z: 4, core: 2. Of those that a mesh axis runs over, the one named last changes fastest.
Arguments:
- gate_in: bfloat16 [1536, 16384], P('ch', 'seg'), may hold values from -6 to 6
- key_in: bfloat16 [1536, 16384], P('ch', 'seg'), may hold values from -6 to 6
- value_in: bfloat16 [1536, 16384], P('ch', 'seg'), may hold values from -6 to 6
- kernel: float32 [1536, 16384], P('ch'), may hold values from -0.046875 to 0.046875
- skip_gain: float32 [1536], P('ch'), may hold values from -1 to 1
- out_weight: bfloat16 [1536, 1536], P('ch'), may hold values from -0.15625 to 0.15625
Outputs:
- output: bfloat16 [16384, 1536], P(('seg', 'ch'))
All inputs are finite; a program needn't handle non-finite values.
Results may differ from a plain program's by a relative error of at most 0.0095.
Values may be sent and summed in bfloat16 or wider, within the bound.
No kernel may reach another device: no remote copies, remote signals or barrier semaphores. Data moves between devices by JAX's collectives and lax.ppermute only.
A program may use at most 128 MiB of HBM per device.

v0:
```python
import math

import jax
import jax.numpy as jnp
from jax import lax
from jax.sharding import PartitionSpec as P

lane_width = 128
highest = lax.Precision.HIGHEST


def angle_pair(height, breadth, period):
    product = (
        jnp.arange(height, dtype=jnp.int32)[:, None]
        * jnp.arange(breadth, dtype=jnp.int32)[None, :]
        % period
    )
    theta = product.astype(jnp.float32) * (2.0 * math.pi / period)
    return (jnp.cos(theta), jnp.sin(theta))


def make_tables(outer):
    cos_outer, sin_outer = angle_pair(outer, outer, outer)
    cos_inner, sin_inner = angle_pair(lane_width, lane_width, lane_width)
    cos_twist, sin_twist = angle_pair(outer, lane_width, outer * lane_width)
    return (cos_outer, sin_outer, cos_inner, sin_inner, cos_twist, sin_twist)


def left_mul(matrix, stack):
    return jnp.einsum("kn,cnm->ckm", matrix, stack, precision=highest)


def right_mul(stack, matrix):
    return jnp.einsum("ckn,nm->ckm", stack, matrix, precision=highest)


def forward(signal, tables):
    cos_outer, sin_outer, cos_inner, sin_inner, cos_twist, sin_twist = tables
    height = signal.shape[1]
    real_a = left_mul(cos_outer[:, :height], signal)
    imag_a = -left_mul(sin_outer[:, :height], signal)
    real_b = real_a * cos_twist + imag_a * sin_twist
    imag_b = imag_a * cos_twist - real_a * sin_twist
    real_x = right_mul(real_b, cos_inner) + right_mul(imag_b, sin_inner)
    imag_x = right_mul(imag_b, cos_inner) - right_mul(real_b, sin_inner)
    return (real_x, imag_x)


def inverse_upper(real_x, imag_x, tables):
    cos_outer, sin_outer, cos_inner, sin_inner, cos_twist, sin_twist = tables
    real_c = right_mul(real_x, cos_inner) - right_mul(imag_x, sin_inner)
    imag_c = right_mul(imag_x, cos_inner) + right_mul(real_x, sin_inner)
    real_d = real_c * cos_twist - imag_c * sin_twist
    imag_d = imag_c * cos_twist + real_c * sin_twist
    middle = cos_outer.shape[0] // 2
    signal = left_mul(cos_outer[middle:], real_d) - left_mul(sin_outer[middle:], imag_d)
    return signal / float(cos_outer.shape[0] * lane_width)


def on_device(gate_in, key_in, value_in, kernel, skip_gain, out_weight):
    seg_index = lax.axis_index("seg")
    col_gate, col_key, col_value = (
        lax.all_to_all(gate_in, "seg", split_axis=0, concat_axis=1, tiled=True),
        lax.all_to_all(key_in, "seg", split_axis=0, concat_axis=1, tiled=True),
        lax.all_to_all(value_in, "seg", split_axis=0, concat_axis=1, tiled=True),
    )
    col_count, full_len = col_key.shape
    long_outer = 2 * full_len // lane_width
    long_tables = make_tables(long_outer)
    first = seg_index * col_count
    my_kernel = lax.dynamic_slice_in_dim(kernel, first, col_count, 0)
    my_skip = lax.dynamic_slice_in_dim(skip_gain, first, col_count, 0)
    col_mixed = col_key.astype(jnp.float32) * col_value.astype(jnp.float32)
    long_filter = jnp.concatenate(
        [jnp.zeros((col_count, full_len), jnp.float32), my_kernel], axis=1
    )
    filt_re, filt_im = forward(long_filter.reshape(col_count, long_outer, lane_width), long_tables)
    sig_re, sig_im = forward(col_mixed.reshape(col_count, long_outer // 2, lane_width), long_tables)
    prod_re = filt_re * sig_re - filt_im * sig_im
    prod_im = filt_re * sig_im + filt_im * sig_re
    col_conv = inverse_upper(prod_re, prod_im, long_tables).reshape(col_count, full_len)
    col_gated = (col_gate.astype(jnp.float32) * (col_conv + my_skip[:, None] * col_mixed)).astype(
        jnp.bfloat16
    )
    gated = lax.all_to_all(col_gated, "seg", split_axis=1, concat_axis=0, tiled=True)
    result = lax.psum_scatter(
        lax.dot_general(
            gated, out_weight, (((0,), (0,)), ((), ())), preferred_element_type=jnp.float32
        ),
        "ch",
        scatter_dimension=0,
        tiled=True,
    )
    return result.astype(jnp.bfloat16)


def solution(mesh):
    placed = (P("ch", "seg"), P("ch", "seg"), P("ch", "seg"), P("ch", None), P("ch"), P("ch", None))
    return jax.shard_map(
        on_device, mesh=mesh, in_specs=placed, out_specs=P(("seg", "ch"), None), check_vma=False
    )
```

profile of v0, /device:TPU:0, one launch (start us, length us, event | category | flops | bytes accessed | tf_op | source)
XLA Modules:
  0.0 486.7 jit_solution(11447293590223693794)
XLA Ops:
  6.5 6.5 %all-to-all-start.1 = ((bf16[4,48,4096]{2,1,0:T(8,128)(2,1)}), bf16[4,48,4096]{2,1,0:T(8,128)(2,1)}, u32[]{:S(2)}, u32[]{:S(2)}) async-start(bf16[4,48,4096]{2,1,0:T(8,128)(2,1)} %bitcast.134), calls=%async_computation.1 | async-start | bytes 3145728 | tf_op jit(solution)/shard_map/all_to_all | solution.py:64
  17.2 11.6 %fusion.44 = f32[48,128,256]{2,1,0:T(8,128)S(1)} fusion(f32[48,256,128]{2,1,0:T(8,128)S(1)} %bitcast.131), kind=kOutput, calls=%fused_computation.51 | convolution fusion | flops 4832755712 | bytes 12582912 | tf_op jit(solution)/shard_map/kn,cnm->ckm/dot_general | solution.py:30
  28.9 21.4 %fusion.46 = f32[48,128,256]{2,1,0:T(8,128)S(1)} fusion(f32[48,256,128]{2,1,0:T(8,128)S(1)} %bitcast.132), kind=kOutput, calls=%fused_computation.53 | convolution fusion | flops 4832755712 | bytes 12582912 | tf_op jit(solution)/shard_map/kn,cnm->ckm/dot_general | solution.py:30
  52.8 12.4 %fusion.23 = f32[48,256,128]{2,1,0:T(8,128)} fusion(f32[48,128,256]{2,1,0:T(8,128)S(1)} %fusion.46, f32[48,128,256]{2,1,0:T(8,128)S(1)} %fusion.44, f32[256,128]{0,1:T(8,128)S(1)} %get-tuple-element.7, f32[256,128]{0,1:T(8,128)S(1)} %get-tuple-element.8), kind=kOutput, calls=%fused_computation.37 | convolution fusion | flops 2422439936 | bytes 19136512 | tf_op jit(solution)/shard_map/ckn,nm->ckm/dot_general | solution.py:34
  72.4 15.9 %fusion.25 = f32[48,256,128]{2,1,0:T(8,128)} fusion(f32[48,128,256]{2,1,0:T(8,128)} %copy-done.3, f32[48,128,256]{2,1,0:T(8,128)} %copy-done.2, f32[256,128]{0,1:T(8,128)S(1)} %get-tuple-element.7, f32[256,128]{0,1:T(8,128)S(1)} %get-tuple-element.8), kind=kOutput, calls=%fused_computation.38 | convolution fusion | flops 2422439936 | bytes 19136512 | tf_op jit(solution)/shard_map/ckn,nm->ckm/dot_general | solution.py:34
  88.3 12.9 %fusion.27 = f32[48,256,128]{2,1,0:T(8,128)} fusion(f32[48,128,256]{2,1,0:T(8,128)S(1)} %bitcast.128, f32[48,128,256]{2,1,0:T(8,128)S(1)} %bitcast.126, f32[256,128]{0,1:T(8,128)S(1)} %get-tuple-element.7, f32[256,128]{0,1:T(8,128)S(1)} %get-tuple-element.8), kind=kOutput, calls=%fused_computation.39 | convolution fusion | flops 2422439936 | bytes 19136512 | tf_op jit(solution)/shard_map/ckn,nm->ckm/dot_general | solution.py:34
  101.1 12.4 %fusion.29 = f32[48,256,128]{2,1,0:T(8,128)} fusion(f32[48,128,256]{2,1,0:T(8,128)S(1)} %bitcast.128, f32[48,128,256]{2,1,0:T(8,128)S(1)} %bitcast.126, f32[256,128]{0,1:T(8,128)S(1)} %get-tuple-element.7, f32[256,128]{0,1:T(8,128)S(1)} %get-tuple-element.8), kind=kOutput, calls=%fused_computation.40 | convolution fusion | flops 2422439936 | bytes 19136512 | tf_op jit(solution)/shard_map/ckn,nm->ckm/dot_general | solution.py:34
  124.7 5.4 %mul.450 = f32[48,128,128]{2,1,0:T(8,128)} reshape(f32[48,4,4096]{2,1,0:T(4,128)} %copy.40) | data formatting | bytes 6291456 | tf_op jit(solution)/shard_map/mul | solution.py:73
  130.1 7.4 %fusion.54 = f32[48,128,256]{2,1,0:T(8,128)S(1)} fusion(f32[48,128,128]{2,1,0:T(8,128)} %mul.450, f32[256,256]{1,0:T(8,128)S(1)} %fusion.58), kind=kOutput, calls=%fused_computation.67 | convolution fusion | flops 2415919104 | bytes 9568256 | tf_op jit(solution)/shard_map/kn,cnm->ckm/dot_general | solution.py:30
  137.6 5.4 %fusion.55 = f32[48,128,256]{2,1,0:T(8,128)S(1)} fusion(f32[48,128,128]{2,1,0:T(8,128)S(1)} %copy-done.5, f32[256,256]{1,0:T(8,128)S(1)} %fusion.59), kind=kOutput, calls=%fused_computation.69 | convolution fusion | flops 2415919104 | bytes 9568256 | tf_op jit(solution)/shard_map/kn,cnm->ckm/dot_general | solution.py:30
  143.0 12.7 %fusion.33 = f32[48,256,128]{2,1,0:T(8,128)} fusion(f32[48,128,256]{2,1,0:T(8,128)S(1)} %fusion.55, f32[48,128,256]{2,1,0:T(8,128)S(1)} %fusion.54, f32[256,128]{0,1:T(8,128)S(1)} %get-tuple-element.7, f32[256,128]{0,1:T(8,128)S(1)} %get-tuple-element.8), kind=kOutput, calls=%fused_computation.42 | convolution fusion | flops 2422439936 | bytes 19136512 | tf_op jit(solution)/shard_map/ckn,nm->ckm/dot_general | solution.py:34
  155.7 12.5 %fusion.37 = f32[48,256,128]{2,1,0:T(8,128)} fusion(f32[48,128,256]{2,1,0:T(8,128)S(1)} %fusion.55, f32[48,128,256]{2,1,0:T(8,128)S(1)} %fusion.54, f32[256,128]{0,1:T(8,128)S(1)} %get-tuple-element.7, f32[256,128]{0,1:T(8,128)S(1)} %get-tuple-element.8), kind=kOutput, calls=%fused_computation.44 | convolution fusion | flops 2422439936 | bytes 19136512 | tf_op jit(solution)/shard_map/ckn,nm->ckm/dot_general | solution.py:34
  168.2 12.9 %fusion.35 = f32[48,256,128]{2,1,0:T(8,128)} fusion(f32[48,128,256]{2,1,0:T(8,128)S(1)} %fusion.55, f32[48,128,256]{2,1,0:T(8,128)S(1)} %fusion.54, f32[256,128]{0,1:T(8,128)S(1)} %get-tuple-element.7, f32[256,128]{0,1:T(8,128)S(1)} %get-tuple-element.8), kind=kOutput, calls=%fused_computation.43 | convolution fusion | flops 2422439936 | bytes 19136512 | tf_op jit(solution)/shard_map/ckn,nm->ckm/dot_general | solution.py:34
  181.1 25.2 %multiply_subtract_fusion = (f32[48,256,128]{2,1,0:T(8,128)}, f32[48,256,128]{2,1,0:T(8,128)}) fusion(f32[48,256,128]{2,1,0:T(8,128)} %fusion.35, f32[48,256,128]{2,1,0:T(8,128)} %fusion.23, f32[48,256,128]{2,1,0:T(8,128)} %fusion.27, f32[48,256,128]{2,1,0:T(8,128)} %fusion.37, f32[48,256,128]{2,1,0:T(8,128)} %fusion.33, f32[48,256,128]{2,1,0:T(8,128)} %fusion.29, ...), kind=kOutput, calls=%fused_computation.21 | convolution fusion | flops 2438168576 | bytes 69468160 | tf_op jit(solution)/shard_map/ckn,nm->ckm/dot_general | solution.py:34
  206.4 9.4 %fusion.68 = f32[48,256,128]{1,2,0:T(8,128)S(1)} fusion(f32[48,256,128]{2,1,0:T(8,128)} %get-tuple-element.6), kind=kOutput, calls=%fused_computation.83 | convolution fusion | flops 2416148480 | bytes 12582912 | tf_op jit(solution)/shard_map/ckn,nm->ckm/dot_general | solution.py:34
  215.8 6.7 %fusion.74 = f32[48,256,128]{1,2,0:T(8,128)S(1)} fusion(f32[48,256,128]{2,1,0:T(8,128)S(1)} %copy-done.4), kind=kOutput, calls=%fused_computation.89 | convolution fusion | flops 2416148480 | bytes 12582912 | tf_op jit(solution)/shard_map/ckn,nm->ckm/dot_general | solution.py:34
  222.5 6.9 %fusion.66 = f32[48,256,128]{1,2,0:T(8,128)S(1)} fusion(f32[48,256,128]{2,1,0:T(8,128)S(1)} %bitcast.130), kind=kOutput, calls=%fused_computation.81 | convolution fusion | flops 2416148480 | bytes 12582912 | tf_op jit(solution)/shard_map/ckn,nm->ckm/dot_general | solution.py:34
  229.4 8.0 %fusion.76 = f32[48,256,128]{1,2,0:T(8,128)} fusion(f32[48,256,128]{2,1,0:T(8,128)S(1)} %bitcast.130), kind=kOutput, calls=%fused_computation.91 | convolution fusion | flops 2416148480 | bytes 12582912 | tf_op jit(solution)/shard_map/ckn,nm->ckm/dot_general | solution.py:34
  237.4 9.0 %fusion.4 = f32[48,128,128]{2,1,0:T(8,128)} fusion(f32[256,128]{0,1:T(8,128)S(1)} %get-tuple-element.7, f32[256,128]{0,1:T(8,128)S(1)} %get-tuple-element.8, f32[48,256,128]{1,2,0:T(8,128)S(1)} %fusion.74, f32[48,256,128]{1,2,0:T(8,128)S(1)} %fusion.66, f32[48,256,128]{1,2,0:T(8,128)} %fusion.76, f32[48,256,128]{1,2,0:T(8,128)S(1)} %fusion.68, ...), kind=kOutput, calls=%fused_computation.12 | convolution fusion | flops 2423783424 | bytes 28704768 | tf_op jit(solution)/shard_map/kn,cnm->ckm/dot_general | solution.py:30
  246.4 9.5 %multiply_bitcast_fusion = f32[48,128,128]{1,2,0:T(8,128)} fusion(f32[48,128,128]{2,1,0:T(8,128)} %fusion.4, f32[256,128]{0,1:T(8,128)S(1)} %get-tuple-element.7, f32[256,128]{0,1:T(8,128)S(1)} %get-tuple-element.8, f32[48,256,128]{1,2,0:T(8,128)S(1)} %fusion.74, f32[48,256,128]{1,2,0:T(8,128)S(1)} %fusion.66, f32[48,256,128]{1,2,0:T(8,128)} %fusion.76, ...), kind=kOutput, calls=%fused_computation.26 | convolution fusion | flops 2425356288 | bytes 31850496 | tf_op jit(solution)/shard_map/kn,cnm->ckm/dot_general | solution.py:30
  264.6 5.7 %fusion.13 = bf16[48,4,4096]{2,0,1:T(8,128)(2,1)S(1)} fusion(f32[48,4,4096]{2,1,0:T(4,128)} %reshape.68, bf16[4,48,4096]{2,1,0:T(8,128)(2,1)} %all-to-all-done, bf16[4,48,4096]{2,1,0:T(8,128)(2,1)} %all-to-all-done.2, bf16[4,48,4096]{2,1,0:T(8,128)(2,1)} %all-to-all-done.1, f32[48]{0:T(128)S(1)} %dynamic_slice.7), kind=kLoop, calls=%fused_computation.25 | loop fusion | flops 6291456 | bytes 9437376 | tf_op jit(solution)/shard_map/convert_element_type | solution.py:82
  270.3 40.2 %all_to_all.55 = bf16[48,4,4096]{2,0,1:T(8,128)(2,1)S(1)} all-to-all(bf16[48,4,4096]{2,0,1:T(8,128)(2,1)S(1)} %fusion.13), channel_id=1, replica_groups=mesh['seg'=4,'ch'=8] {'seg'}, dimensions={1} | all-to-all | bytes 3145728 | tf_op jit(solution)/shard_map/all_to_all | solution.py:85
  310.5 10.1 %fusion.157 = f32[4096,1536]{1,0:T(8,128)} fusion(bf16[192,4096]{1,0:T(8,128)(2,1)S(1)} %bitcast.133, bf16[192,1536]{1,0:T(8,128)(2,1)S(1)} %copy-done), kind=kOutput, calls=%fused_computation.161 | convolution fusion | flops 2415919104 | bytes 27328512 | tf_op jit(solution)/shard_map/dot_general | solution.py:87
  320.7 155.6 %reduce-scatter.2.cloned.1.call-done = f32[512,1536]{1,0:T(8,128)} async-done(((f32[4096,1536]{1,0:T(8,128)}), f32[512,1536]{1,0:T(8,128)}) %reduce-scatter.2.cloned.1.call-update) | async-done | bytes 3145744 | tf_op jit(solution)/shard_map/reduce_scatter | solution.py:86
  (48 shorter events, 36.9 us)
Async XLA Ops:
  6.5 304.0 %copy-start = (bf16[192,1536]{1,0:T(8,128)(2,1)S(1)}, bf16[192,1536]{1,0:T(8,128)(2,1)}, u32[]{:S(2)}) copy-start(bf16[192,1536]{1,0:T(8,128)(2,1)} %param.11) | copy-start | bytes 1769476
  6.5 58.7 %all-to-all-start.1 = ((bf16[4,48,4096]{2,1,0:T(8,128)(2,1)}), bf16[4,48,4096]{2,1,0:T(8,128)(2,1)}, u32[]{:S(2)}, u32[]{:S(2)}) async-start(bf16[4,48,4096]{2,1,0:T(8,128)(2,1)} %bitcast.134), calls=%async_computation.1 | async-start | bytes 3145728 | tf_op jit(solution)/shard_map/all_to_all | solution.py:64
  15.5 1.1 copy-start.6
  28.8 21.4 %copy-start.2 = (f32[48,128,256]{2,1,0:T(8,128)}, f32[48,128,256]{2,1,0:T(8,128)S(1)}, u32[]{:S(2)}) copy-start(f32[48,128,256]{2,1,0:T(8,128)S(1)} %fusion.44) | copy-start | bytes 18874372
  50.3 2.6 copy-start.3
  65.3 48.3 %all-to-all-start.2 = ((bf16[4,48,4096]{2,1,0:T(8,128)(2,1)}), bf16[4,48,4096]{2,1,0:T(8,128)(2,1)}, u32[]{:S(2)}, u32[]{:S(2)}) async-start(bf16[4,48,4096]{2,1,0:T(8,128)(2,1)} %bitcast.135), calls=%async_computation.2 | async-start | bytes 3145728 | tf_op jit(solution)/shard_map/all_to_all | solution.py:65
  71.3 16.9 %slice-start = ((s8[6291456]{0:T(1024)(128)(4,1)}), s8[4194304]{0:T(1024)(128)(4,1)S(1)}, s32[]{:S(2)}) async-start(s8[6291456]{0:T(1024)(128)(4,1)} %bitcast.125), calls=%async_computation.6 | async-start | bytes 8388608
  71.4 16.9 %slice-start.2 = ((s8[6291456]{0:T(1024)(128)(4,1)}), s8[4194304]{0:T(1024)(128)(4,1)S(1)}, s32[]{:S(2)}) async-start(s8[6291456]{0:T(1024)(128)(4,1)} %bitcast.127), calls=%async_computation.8 | async-start | bytes 8388608
  72.3 15.9 %slice-start.1 = ((s8[6291456]{0:T(1024)(128)(4,1)}), s8[2097152]{0:T(1024)(128)(4,1)S(1)}, s32[]{:S(2)}) async-start(s8[6291456]{0:T(1024)(128)(4,1)} %bitcast.125), calls=%async_computation.7 | async-start | bytes 4194304
  72.3 15.9 %slice-start.3 = ((s8[6291456]{0:T(1024)(128)(4,1)}), s8[2097152]{0:T(1024)(128)(4,1)S(1)}, s32[]{:S(2)}) async-start(s8[6291456]{0:T(1024)(128)(4,1)} %bitcast.127), calls=%async_computation.9 | async-start | bytes 4194304
  113.6 151.1 %all-to-all-start = ((bf16[4,48,4096]{2,1,0:T(8,128)(2,1)}), bf16[4,48,4096]{2,1,0:T(8,128)(2,1)}, u32[]{:S(2)}, u32[]{:S(2)}) async-start(bf16[4,48,4096]{2,1,0:T(8,128)(2,1)} %bitcast.136), calls=%async_computation | async-start | bytes 3145728 | tf_op jit(solution)/shard_map/all_to_all | solution.py:63
  118.7 357.6 %reduce-scatter.2.cloned.1.call-start = ((), (), s32[]{:S(2)}) async-start(), calls=%async_computation.5 | async-start | bytes 28311552 | tf_op jit(solution)/shard_map/reduce_scatter | solution.py:86
  130.1 7.5 %copy-start.5 = (f32[48,128,128]{2,1,0:T(8,128)S(1)}, f32[48,128,128]{2,1,0:T(8,128)}, u32[]{:S(2)}) copy-start(f32[48,128,128]{2,1,0:T(8,128)} %mul.450) | copy-start | bytes 9437188
  143.0 25.2 %copy-start.1 = (f32[48,128,256]{2,1,0:T(8,128)}, f32[48,128,256]{2,1,0:T(8,128)S(1)}, u32[]{:S(2)}) copy-start(f32[48,128,256]{2,1,0:T(8,128)S(1)} %fusion.55) | copy-start | bytes 18874372
  206.4 9.4 %copy-start.4 = (f32[48,256,128]{2,1,0:T(8,128)S(1)}, f32[48,256,128]{2,1,0:T(8,128)}, u32[]{:S(2)}) copy-start(f32[48,256,128]{2,1,0:T(8,128)} %get-tuple-element.6) | copy-start | bytes 18874372
  206.4 16.1 %slice-start.4 = ((s8[6291456]{0:T(1024)(128)(4,1)}), s8[4194304]{0:T(1024)(128)(4,1)S(1)}, s32[]{:S(2)}) async-start(s8[6291456]{0:T(1024)(128)(4,1)} %bitcast.129), calls=%async_computation.10 | async-start | bytes 8388608
  215.8 6.7 %slice-start.5 = ((s8[6291456]{0:T(1024)(128)(4,1)}), s8[2097152]{0:T(1024)(128)(4,1)S(1)}, s32[]{:S(2)}) async-start(s8[6291456]{0:T(1024)(128)(4,1)} %bitcast.129), calls=%async_computation.11 | async-start | bytes 4194304
Sparse Core Ops, SparseCore 0:
  320.8 155.3 reduce-scatter.1
where the time goes:
time: 496 us; the launch traced here: 487 us
  matrix products  222 us (45%)
  waiting for transfers between devices  156 us (31%)
  blocking collectives  40.2 us (8%)
  local copies, waits for them, and re-layouts  24.1 us (5%)
  starting transfers between devices  16.7 us (3%)
  between operations  14.1 us (3%)
  other arithmetic  13.6 us (3%)
    reduce_scatter x1, waiting for transfers between devices, on_device(): lax.psum_scatter(lax.dot_general(gated, out_weight, (((0,), (0,)), ((), (...  156 us
    dot_general x12, matrix products, right_mul(): return jnp.einsum('ckn,nm->ckm', stack, matrix, precision=highest)  148 us
    dot_general x6, matrix products, left_mul(): return jnp.einsum('kn,cnm->ckm', matrix, stack, precision=highest)  64.4 us
    all_to_all x1, blocking collectives, on_device(): lax.all_to_all(col_gated, 'seg', split_axis=1, concat_axis=0, tiled=True)  40.2 us
    dot_general x1, matrix products, on_device(): lax.dot_general(gated, out_weight, (((0,), (0,)), ((), ())), preferred_el...  10.1 us
  transfers between devices with their start and end apart: 4, of which 1 were waited for; matrix products, arithmetic and copies ran while one was open for 49% of the time, Pallas kernels for 0%

commit v1 on v0

v1 whole, which is shorter than its diff:
```python
import math
from functools import partial

import jax
import jax.numpy as jnp
import numpy as np
from jax import lax
from jax.experimental import pallas as pl
from jax.experimental.pallas import tpu as pltpu
from jax.sharding import PartitionSpec as P

lane_width = 128
row_pad = 8
f32 = jnp.float32
bf16 = jnp.bfloat16


def make_tables(rows):
    length = rows * lane_width
    k1 = np.arange(rows)[:, None] + 0.25
    outer = 2.0 * math.pi * (k1 * np.arange(rows)[None, :]) / rows
    twist = 2.0 * math.pi * (k1 * np.arange(lane_width)[None, :]) / length
    lanes = np.arange(lane_width)
    inner = 2.0 * math.pi * (lanes[:, None] * lanes[None, :] % lane_width) / lane_width
    cos_i, sin_i = np.cos(inner), np.sin(inner)
    outer_fwd = np.concatenate([np.cos(outer), -np.sin(outer)], 0)
    inner_fwd = np.block([[cos_i, -sin_i], [sin_i, cos_i]])
    inner_inv = np.block([[cos_i, sin_i], [-sin_i, cos_i]])
    outer_inv = np.concatenate([np.cos(outer.T), -np.sin(outer.T)], 1) / length
    mats = tuple(jnp.asarray(m, dtype=bf16) for m in (outer_fwd, inner_fwd, inner_inv, outer_inv))
    return mats, (jnp.asarray(np.cos(twist), f32), jnp.asarray(-np.sin(twist), f32))


def mm(a, b):
    return jnp.dot(a, b, preferred_element_type=f32)


def forward(read, members, rows, outer_fwd, inner_fwd, tw_re, tw_im):
    side = jnp.concatenate([read(g) for g in members], axis=1).astype(bf16)
    a = mm(outer_fwd, side)
    parts = []
    for i in range(len(members)):
        re = a[:rows, i * lane_width : (i + 1) * lane_width]
        im = a[rows:, i * lane_width : (i + 1) * lane_width]
        parts.append(jnp.concatenate([re * tw_re - im * tw_im, re * tw_im + im * tw_re], axis=1))
    return mm(jnp.concatenate(parts, axis=0).astype(bf16), inner_fwd)


def members_of(count):
    width = 2 if count % 2 == 0 else 1
    return [tuple(range(g, g + width)) for g in range(0, count, width)]


def filter_body(rows, count, k_ref, of_ref, if_ref, tr_ref, ti_ref, out_ref, rows_s):
    pitch = rows + row_pad
    for r in range(rows):
        rows_s[pl.ds(r, count, stride=pitch), :] = k_ref[:, r * lane_width : (r + 1) * lane_width]
    read = lambda g: rows_s[pl.ds(g * pitch, rows), :]
    for members in members_of(count):
        spec = forward(read, members, rows, of_ref[...], if_ref[...], tr_ref[...], ti_ref[...])
        out_ref[pl.ds(members[0] * rows, len(members) * rows), :] = spec


def conv_body(rows, count, segs, u_ref, h_ref, of_ref, if_ref, ii_ref, oi_ref, tr_ref, ti_ref, out_ref, in_s, out_s):
    pitch = rows + row_pad
    per = rows // segs
    for r in range(rows):
        s, q = divmod(r, per)
        in_s[pl.ds(r, count, stride=pitch), :] = u_ref[s, :, q * lane_width : (q + 1) * lane_width].astype(f32)
    read = lambda g: in_s[pl.ds(g * pitch, rows), :]
    tw_re, tw_im = tr_ref[...], ti_ref[...]
    for members in members_of(count):
        x = forward(read, members, rows, of_ref[...], if_ref[...], tw_re, tw_im)
        h = h_ref[pl.ds(members[0] * rows, len(members) * rows), :]
        xr, xi = x[:, :lane_width], x[:, lane_width:]
        hr, hi = h[:, :lane_width], h[:, lane_width:]
        prod = jnp.concatenate([hr * xr - hi * xi, hr * xi + hi * xr], axis=1).astype(bf16)
        c = mm(prod, ii_ref[...])
        cols = []
        for i in range(len(members)):
            cr = c[i * rows : (i + 1) * rows, :lane_width]
            ci = c[i * rows : (i + 1) * rows, lane_width:]
            cols.append(jnp.concatenate([cr * tw_re + ci * tw_im, ci * tw_re - cr * tw_im], axis=0))
        y = mm(oi_ref[...], jnp.concatenate(cols, axis=1).astype(bf16))
        for i, g in enumerate(members):
            out_s[pl.ds(g * pitch, rows), :] = y[:, i * lane_width : (i + 1) * lane_width]
    for r in range(rows):
        s, q = divmod(r, per)
        out_ref[s, :, q * lane_width : (q + 1) * lane_width] = out_s[pl.ds(r, count, stride=pitch), :].astype(bf16)


def whole(array):
    return pl.BlockSpec(array.shape, lambda *_: (0,) * array.ndim)


def filter_call(my_kernel, step, chunk, mats, twists):
    full = my_kernel.shape[1]
    rows = full // lane_width
    consts = (mats[0], mats[1], *twists)
    return pl.pallas_call(
        partial(filter_body, rows, step),
        grid=(1,),
        in_specs=[pl.BlockSpec((step, full), lambda i: (chunk, 0)), *map(whole, consts)],
        out_specs=pl.BlockSpec((step * rows, 2 * lane_width), lambda i: (i, 0)),
        out_shape=jax.ShapeDtypeStruct((step * rows, 2 * lane_width), f32),
        scratch_shapes=[pltpu.VMEM((step * (rows + row_pad), lane_width), f32)],
        compiler_params=pltpu.CompilerParams(vmem_limit_bytes=40 << 20),
        cost_estimate=pl.CostEstimate(flops=step * rows * 3 * rows * 4 * lane_width, transcendentals=0, bytes_accessed=step * full * 12),
        name="filter_spectrum",
    )(my_kernel, *consts)


def conv_call(streams, spectrum, mats, twists):
    segs, step, part = streams.shape
    full = segs * part
    rows = full // lane_width
    consts = (*mats, *twists)
    pad_rows = step * (rows + row_pad)
    return pl.pallas_call(
        partial(conv_body, rows, step, segs),
        grid=(1,),
        in_specs=[
            pl.BlockSpec((segs, step, part), lambda i: (0, 0, 0)),
            pl.BlockSpec((step * rows, 2 * lane_width), lambda i: (0, 0)),
            *map(whole, consts),
        ],
        out_specs=pl.BlockSpec((segs, step, part), lambda i: (0, 0, 0)),
        out_shape=jax.ShapeDtypeStruct((segs, step, part), bf16),
        scratch_shapes=[pltpu.VMEM((pad_rows, lane_width), f32), pltpu.VMEM((pad_rows, lane_width), f32)],
        compiler_params=pltpu.CompilerParams(vmem_limit_bytes=40 << 20),
        cost_estimate=pl.CostEstimate(flops=step * rows * 6 * rows * 4 * lane_width, transcendentals=0, bytes_accessed=step * full * 12),
        name="long_conv",
    )(streams, spectrum, *consts)


def on_device(gate_in, key_in, value_in, kernel, skip_gain, out_weight):
    segs = lax.axis_size("seg")
    groups = lax.axis_size("ch")
    held, part = key_in.shape
    full = kernel.shape[1]
    width = out_weight.shape[1]
    col = held // segs
    step = 16 if col % 16 == 0 else col
    chunks = col // step
    mats, twists = make_tables(full // lane_width)

    def cut(array):
        return array.reshape(segs, chunks, step, *array.shape[1:])

    key_c, value_c, gate_c, skip_c = map(cut, (key_in, value_in, gate_in, skip_gain))

    def mixed(j):
        return key_c[:, j].astype(f32) * value_c[:, j].astype(f32)

    swap = partial(lax.all_to_all, split_axis=0, concat_axis=0, tiled=True)
    arrived = [swap(mixed(j).astype(bf16), "seg") for j in range(chunks)]
    my_kernel = lax.dynamic_slice_in_dim(kernel, lax.axis_index("seg") * col, col, 0)
    spectra = [filter_call(my_kernel, step, j, mats, twists) for j in range(chunks)]
    weights = lax.all_gather(out_weight, "ch", axis=0, tiled=True)
    weights = weights.reshape(groups, segs, chunks, step, width)
    result = None
    for j in range(chunks):
        convolved = swap(conv_call(arrived[j], spectra[j], mats, twists), "seg")
        gated = (
            gate_c[:, j].astype(f32) * (convolved.astype(f32) + skip_c[:, j, :, None] * mixed(j))
        ).astype(bf16)
        tokens = gated.reshape(segs * step, groups, part // groups).transpose(1, 0, 2)
        mine = swap(tokens, "ch").reshape(groups * segs * step, part // groups)
        share = lax.dot_general(
            mine,
            weights[:, :, j].reshape(groups * segs * step, width),
            (((0,), (0,)), ((), ())),
            preferred_element_type=f32,
        )
        result = share if result is None else result + share
    return result.astype(bf16)


def solution(mesh):
    placed = (P("ch", "seg"), P("ch", "seg"), P("ch", "seg"), P("ch", None), P("ch"), P("ch", None))
    return jax.shard_map(
        on_device, mesh=mesh, in_specs=placed, out_specs=P(("seg", "ch"), None), check_vma=False
    )
```

time: 496 us -> 178 us (0.36); the launches traced: 487 us -> 177 us
  matrix products: 222 us -> 6.82 us
  waiting for transfers between devices: 156 us -> 66.9 us
  blocking collectives: 40.2 us -> 20.7 us
  Pallas kernels: 0 us -> 18.1 us
  starting transfers between devices: 16.7 us -> 30.9 us
  local copies, waits for them, and re-layouts: 24.1 us -> 13.2 us
  other arithmetic: 13.6 us -> 6.63 us
    dot_general x19 -> x3, matrix products: 222 us -> 6.82 us  [on_device(): lax.dot_general(mine, weights[:, :, j].reshape(groups * segs * step, widt...]
    reduce_scatter x1 -> x0, waiting for transfers between devices: 156 us -> none  [on_device(): lax.psum_scatter(lax.dot_general(gated, out_weight, (((0,), (0,)), ((), (...]
    all_to_all x3 -> x8, waiting for transfers between devices: 0.01 us -> 66.1 us  [the longest x3 28.2 us: on_device(): convolved = swap(conv_call(arrived[j], spectra[j], mats, twists), 'seg')]
    all_to_all x1, blocking collectives: 40.2 us -> 20.7 us  [on_device(): arrived = [swap(mixed(j).astype(bf16), 'seg') for j in range(chunks)]]
    pallas_call x0 -> x6, Pallas kernels: none -> 18.1 us  [the longest x3 15.4 us: conv_call(): pl.pallas_call(partial(conv_body, rows, step, segs), grid=(1,), in_specs=...]
    all_to_all x3 -> x8, starting transfers between devices: 16.7 us -> 30.9 us  [the longest x3 11.9 us: on_device(): convolved = swap(conv_call(arrived[j], spectra[j], mats, twists), 'seg')]
    mul x2 -> x0, local copies, waits for them, and re-layouts: 9.1 us -> none  [on_device(): col_mixed = col_key.astype(jnp.float32) * col_value.astype(jnp.float32)]
  transfers between devices with their start and end apart: 4 -> 9, of which waited for: 1 -> 8; matrix products, arithmetic and copies ran while one was open for 49% -> 11% of each run, Pallas kernels for 0% -> 10%
where the time goes in v1:
time: 178 us; the launch traced here: 177 us
  waiting for transfers between devices  66.9 us (38%)
  starting transfers between devices  30.9 us (17%)
  blocking collectives  20.7 us (12%)
  Pallas kernels  18.1 us (10%)
  between operations  13.7 us (8%)
  local copies, waits for them, and re-layouts  13.2 us (7%)
  matrix products  6.82 us (4%)
  other arithmetic  6.63 us (4%)
    all_to_all x3, waiting for transfers between devices, on_device(): convolved = swap(conv_call(arrived[j], spectra[j], mats, twists), 'seg')  28.2 us
    all_to_all x1, blocking collectives, on_device(): arrived = [swap(mixed(j).astype(bf16), 'seg') for j in range(chunks)]  20.7 us
    all_to_all x2, waiting for transfers between devices, on_device(): arrived = [swap(mixed(j).astype(bf16), 'seg') for j in range(chunks)]  19.2 us
    all_to_all x3, waiting for transfers between devices, on_device(): mine = swap(tokens, 'ch').reshape(groups * segs * step, part // groups)  18.8 us
    pallas_call x3, Pallas kernels, conv_call(): pl.pallas_call(partial(conv_body, rows, step, segs), grid=(1,), in_specs=...  15.4 us
    all_to_all x3, starting transfers between devices, on_device(): convolved = swap(conv_call(arrived[j], spectra[j], mats, twists), 'seg')  11.9 us
    all_to_all x3, starting transfers between devices, on_device(): mine = swap(tokens, 'ch').reshape(groups * segs * step, part // groups)  11.4 us
    all_to_all x2, starting transfers between devices, on_device(): arrived = [swap(mixed(j).astype(bf16), 'seg') for j in range(chunks)]  7.61 us
  transfers between devices with their start and end apart: 9, of which 8 were waited for; matrix products, arithmetic and copies ran while one was open for 11% of the time, Pallas kernels for 10%

profile of v1, /device:TPU:0, one launch (start us, length us, event | category | flops | bytes accessed | tf_op | source)
XLA Modules:
  0.0 177.0 jit_solution(15061278656782274055)
XLA Ops:
  7.3 3.3 %bitcast_convert_fusion = (bf16[4,16,4096]{2,1,0:T(8,128)(2,1)}, bf16[4,16,4096]{2,1,0:T(8,128)(2,1)}, bf16[4,16,4096]{2,1,0:T(8,128)(2,1)S(1)}) fusion(bf16[4,3,16,4096]{3,2,1,0:T(8,128)(2,1)} %bitcast.118, bf16[4,3,16,4096]{3,2,1,0:T(8,128)(2,1)} %bitcast.120), kind=kLoop, calls=%fused_computation.10 | loop fusion | flops 3145728 | bytes 4718592 | tf_op jit(solution)/shard_map/convert_element_type | solution.py:156
  10.6 20.7 %all_to_all.45.u_ref = bf16[4,16,4096]{2,1,0:T(8,128)(2,1)} all-to-all(bf16[4,16,4096]{2,1,0:T(8,128)(2,1)S(1)} %get-tuple-element.13), channel_id=1, replica_groups=mesh['seg'=4,'ch'=8] {'seg'}, dimensions={0} | all-to-all | bytes 1048576 | tf_op jit(solution)/shard_map/all_to_all | solution.py:156
  31.3 3.5 %all-to-all-start.3 = ((bf16[4,16,4096]{2,1,0:T(8,128)(2,1)}), bf16[4,16,4096]{2,1,0:T(8,128)(2,1)S(1)}, u32[]{:S(2)}, u32[]{:S(2)}) async-start(bf16[4,16,4096]{2,1,0:T(8,128)(2,1)} %get-tuple-element.12), calls=%async_computation.3 | async-start | bytes 1048576 | tf_op jit(solution)/shard_map/all_to_all | solution.py:156
  34.8 13.7 %all-to-all-done.3.u_ref = bf16[4,16,4096]{2,1,0:T(8,128)(2,1)S(1)} async-done(((bf16[4,16,4096]{2,1,0:T(8,128)(2,1)}), bf16[4,16,4096]{2,1,0:T(8,128)(2,1)S(1)}, u32[]{:S(2)}, u32[]{:S(2)}) %all-to-all-start.3) | async-done | bytes 524320 | tf_op jit(solution)/shard_map/all_to_all | solution.py:156
  49.3 4.1 %all-to-all-start.6 = ((bf16[4,16,4096]{2,1,0:T(8,128)(2,1)}), bf16[4,16,4096]{2,1,0:T(8,128)(2,1)}, u32[]{:S(2)}, u32[]{:S(2)}) async-start(bf16[4,16,4096]{2,1,0:T(8,128)(2,1)} %get-tuple-element.11), calls=%async_computation.6 | async-start | bytes 1048576 | tf_op jit(solution)/shard_map/all_to_all | solution.py:156
  56.7 4.5 %long_conv.3 = bf16[4,16,4096]{2,1,0:T(8,128)(2,1)S(1)} custom-call(bf16[4,16,4096]{2,1,0:T(8,128)(2,1)S(1)} %copy-done.6, f32[2048,256]{1,0:T(8,128)S(1)} %filter_spectrum.3.h_ref, bf16[256,128]{1,0:T(8,128)(2,1)S(1)} %copy-done.1, bf16[256,256]{1,0:T(8,128)(2,1)S(1)} %copy-done, bf16[256,256]{1,0:T(8,128)(2,1)S(1)} %copy-done.9, ...), custom_call_target="tpu_custom_call" | custom-call | flops 805306368 | bytes 3145728 | tf_op jit(solution)/shard_map/long_conv/pallas_call | solution.py:119
  62.0 5.5 %all-to-all-done.6.u_ref = bf16[4,16,4096]{2,1,0:T(8,128)(2,1)} async-done(((bf16[4,16,4096]{2,1,0:T(8,128)(2,1)}), bf16[4,16,4096]{2,1,0:T(8,128)(2,1)}, u32[]{:S(2)}, u32[]{:S(2)}) %all-to-all-start.6) | async-done | bytes 524320 | tf_op jit(solution)/shard_map/all_to_all | solution.py:156
  67.5 4.1 %all-to-all-start.1 = ((bf16[4,16,4096]{2,1,0:T(8,128)(2,1)}), bf16[4,16,4096]{2,1,0:T(8,128)(2,1)}, u32[]{:S(2)}, u32[]{:S(2)}) async-start(bf16[4,16,4096]{2,1,0:T(8,128)(2,1)} %copy-done.8), calls=%async_computation.1 | async-start | bytes 1048576 | tf_op jit(solution)/shard_map/all_to_all | solution.py:163
  72.7 4.5 %long_conv.4 = bf16[4,16,4096]{2,1,0:T(8,128)(2,1)S(1)} custom-call(bf16[4,16,4096]{2,1,0:T(8,128)(2,1)S(1)} %copy-done.5, f32[2048,256]{1,0:T(8,128)S(1)} %filter_spectrum.4.h_ref, bf16[256,128]{1,0:T(8,128)(2,1)S(1)} %copy-done.1, bf16[256,256]{1,0:T(8,128)(2,1)S(1)} %copy-done, bf16[256,256]{1,0:T(8,128)(2,1)S(1)} %copy-done.10, ...), custom_call_target="tpu_custom_call" | custom-call | flops 805306368 | bytes 3145728 | tf_op jit(solution)/shard_map/long_conv/pallas_call | solution.py:119
  78.0 7.8 %all-to-all-done.1 = bf16[4,16,4096]{2,1,0:T(8,128)(2,1)} async-done(((bf16[4,16,4096]{2,1,0:T(8,128)(2,1)}), bf16[4,16,4096]{2,1,0:T(8,128)(2,1)}, u32[]{:S(2)}, u32[]{:S(2)}) %all-to-all-start.1) | async-done | bytes 524320 | tf_op jit(solution)/shard_map/all_to_all | solution.py:163
  85.8 4.1 %all-to-all-start.4 = ((bf16[4,16,4096]{2,1,0:T(8,128)(2,1)}), bf16[4,16,4096]{2,1,0:T(8,128)(2,1)}, u32[]{:S(2)}, u32[]{:S(2)}) async-start(bf16[4,16,4096]{2,1,0:T(8,128)(2,1)} %copy-done.7), calls=%async_computation.4 | async-start | bytes 1048576 | tf_op jit(solution)/shard_map/all_to_all | solution.py:163
  90.9 6.4 %long_conv.5 = bf16[4,16,4096]{2,1,0:T(8,128)(2,1)} custom-call(bf16[4,16,4096]{2,1,0:T(8,128)(2,1)} %all-to-all-done.6.u_ref, f32[2048,256]{1,0:T(8,128)S(1)} %filter_spectrum.5.h_ref, bf16[256,128]{1,0:T(8,128)(2,1)S(1)} %copy-done.1, bf16[256,256]{1,0:T(8,128)(2,1)S(1)} %copy-done, bf16[256,256]{1,0:T(8,128)(2,1)S(1)} %copy-done.11, ...), custom_call_target="tpu_custom_call" | custom-call | flops 805306368 | bytes 3145728 | tf_op jit(solution)/shard_map/long_conv/pallas_call | solution.py:119
  97.3 6.7 %all-to-all-done.4 = bf16[4,16,4096]{2,1,0:T(8,128)(2,1)} async-done(((bf16[4,16,4096]{2,1,0:T(8,128)(2,1)}), bf16[4,16,4096]{2,1,0:T(8,128)(2,1)}, u32[]{:S(2)}, u32[]{:S(2)}) %all-to-all-start.4) | async-done | bytes 524320 | tf_op jit(solution)/shard_map/all_to_all | solution.py:163
  104.0 3.7 %all-to-all-start.7 = ((bf16[4,16,4096]{2,1,0:T(8,128)(2,1)}), bf16[4,16,4096]{2,1,0:T(8,128)(2,1)S(1)}, u32[]{:S(2)}, u32[]{:S(2)}) async-start(bf16[4,16,4096]{2,1,0:T(8,128)(2,1)} %long_conv.5), calls=%async_computation.7 | async-start | bytes 1048576 | tf_op jit(solution)/shard_map/all_to_all | solution.py:163
  107.8 13.7 %all-to-all-done.7 = bf16[4,16,4096]{2,1,0:T(8,128)(2,1)S(1)} async-done(((bf16[4,16,4096]{2,1,0:T(8,128)(2,1)}), bf16[4,16,4096]{2,1,0:T(8,128)(2,1)S(1)}, u32[]{:S(2)}, u32[]{:S(2)}) %all-to-all-start.7) | async-done | bytes 524320 | tf_op jit(solution)/shard_map/all_to_all | solution.py:163
  121.5 3.3 %fusion.1 = (bf16[4,16,4096]{2,1,0:T(8,128)(2,1)S(1)}, bf16[4,16,4096]{2,1,0:T(8,128)(2,1)S(1)}, bf16[4,16,4096]{2,1,0:T(8,128)(2,1)S(1)}) fusion(bf16[4,16,4096]{2,1,0:T(8,128)(2,1)S(1)} %all-to-all-done.7, bf16[4,3,16,4096]{3,2,1,0:T(8,128)(2,1)} %bitcast.131, f32[4,16]{1,0:T(4,128)S(1)} %bitcast.132, bf16[4,3,16,4096]{3,2,1,0:T(8,128)(2,1)S(1)} %bitcast.119, ...), kind=kLoop, calls=%fused_computation.4 | loop fusion | flops 7077888 | bytes 7865088 | tf_op jit(solution)/shard_map/convert_element_type | solution.py:166
  126.0 3.7 %all-to-all-start.2 = ((bf16[8,64,512]{2,1,0:T(8,128)(2,1)}), bf16[8,64,512]{2,1,0:T(8,128)(2,1)S(1)}, u32[]{:S(2)}, u32[]{:S(2)}) async-start(bf16[8,64,512]{2,1,0:T(8,128)(2,1)} %bitcast.114), calls=%async_computation.2 | async-start | bytes 1048576 | tf_op jit(solution)/shard_map/all_to_all | solution.py:168
  131.9 7.5 %all-to-all-done.2 = bf16[8,64,512]{2,1,0:T(8,128)(2,1)S(1)} async-done(((bf16[8,64,512]{2,1,0:T(8,128)(2,1)}), bf16[8,64,512]{2,1,0:T(8,128)(2,1)S(1)}, u32[]{:S(2)}, u32[]{:S(2)}) %all-to-all-start.2) | async-done | bytes 524320 | tf_op jit(solution)/shard_map/all_to_all | solution.py:168
  139.4 3.5 %all-to-all-start.5 = ((bf16[8,64,512]{2,1,0:T(8,128)(2,1)}), bf16[8,64,512]{2,1,0:T(8,128)(2,1)S(1)}, u32[]{:S(2)}, u32[]{:S(2)}) async-start(bf16[8,64,512]{2,1,0:T(8,128)(2,1)} %bitcast.113), calls=%async_computation.5 | async-start | bytes 1048576 | tf_op jit(solution)/shard_map/all_to_all | solution.py:168
  142.9 4.5 %fusion.7 = (bf16[8,4,1,16,1536]{4,3,2,1,0:T(8,128)(2,1)}, bf16[8,4,1,16,1536]{4,3,2,1,0:T(8,128)(2,1)}, bf16[8,4,1,16,1536]{4,3,2,1,0:T(8,128)(2,1)S(1)}) fusion(bf16[8,4,3,16,1536]{4,3,2,1,0:T(8,128)(2,1)} %bitcast.122), kind=kLoop, calls=%fused_computation.34 | loop fusion | bytes 9437184 | tf_op jit(solution)/shard_map/slice | solution.py:171
  147.5 5.1 %all-to-all-done.5 = bf16[8,64,512]{2,1,0:T(8,128)(2,1)S(1)} async-done(((bf16[8,64,512]{2,1,0:T(8,128)(2,1)}), bf16[8,64,512]{2,1,0:T(8,128)(2,1)S(1)}, u32[]{:S(2)}, u32[]{:S(2)}) %all-to-all-start.5) | async-done | bytes 524320 | tf_op jit(solution)/shard_map/all_to_all | solution.py:168
  152.5 4.1 %all-to-all-start.8 = ((bf16[8,64,512]{2,1,0:T(8,128)(2,1)}), bf16[8,64,512]{2,1,0:T(8,128)(2,1)}, u32[]{:S(2)}, u32[]{:S(2)}) async-start(bf16[8,64,512]{2,1,0:T(8,128)(2,1)} %bitcast.112), calls=%async_computation.8 | async-start | bytes 1048576 | tf_op jit(solution)/shard_map/all_to_all | solution.py:168
  160.2 6.2 %all-to-all-done.8 = bf16[8,64,512]{2,1,0:T(8,128)(2,1)} async-done(((bf16[8,64,512]{2,1,0:T(8,128)(2,1)}), bf16[8,64,512]{2,1,0:T(8,128)(2,1)}, u32[]{:S(2)}, u32[]{:S(2)}) %all-to-all-start.8) | async-done | bytes 524320 | tf_op jit(solution)/shard_map/all_to_all | solution.py:168
  166.4 3.7 %fusion = bf16[512,1536]{1,0:T(8,128)(2,1)} fusion(f32[512,1536]{1,0:T(8,128)S(1)} %convolution_add_fusion.1, bf16[512,512]{1,0:T(8,128)(2,1)} %bitcast.20, bf16[512,1536]{1,0:T(8,128)(2,1)} %bitcast.116), kind=kOutput, calls=%fused_computation.2 | convolution fusion | flops 806879232 | bytes 6815744 | tf_op jit(solution)/shard_map/dot_general | solution.py:169
  (51 shorter events, 15.3 us)
Async XLA Ops:
  6.5 136.4 %all-gather.2.cloned.1.call-start = ((), (), s32[]{:S(2)}) async-start(), calls=%async_computation.9 | async-start | bytes 5308416 | tf_op jit(solution)/shard_map/all_gather | solution.py:159
  31.3 17.1 %all-to-all-start.3 = ((bf16[4,16,4096]{2,1,0:T(8,128)(2,1)}), bf16[4,16,4096]{2,1,0:T(8,128)(2,1)S(1)}, u32[]{:S(2)}, u32[]{:S(2)}) async-start(bf16[4,16,4096]{2,1,0:T(8,128)(2,1)} %get-tuple-element.12), calls=%async_computation.3 | async-start | bytes 1048576 | tf_op jit(solution)/shard_map/all_to_all | solution.py:156
  48.4 0.8 copy-start.4
  49.3 18.3 %all-to-all-start.6 = ((bf16[4,16,4096]{2,1,0:T(8,128)(2,1)}), bf16[4,16,4096]{2,1,0:T(8,128)(2,1)}, u32[]{:S(2)}, u32[]{:S(2)}) async-start(bf16[4,16,4096]{2,1,0:T(8,128)(2,1)} %get-tuple-element.11), calls=%async_computation.6 | async-start | bytes 1048576 | tf_op jit(solution)/shard_map/all_to_all | solution.py:156
  53.4 2.2 %copy-start = (bf16[256,256]{1,0:T(8,128)(2,1)S(1)}, bf16[256,256]{1,0:T(8,128)(2,1)}, u32[]{:S(2)}) copy-start(bf16[256,256]{1,0:T(8,128)(2,1)} %constant.24.clone.if_ref) | copy-start | bytes 393220
  53.4 2.2 %copy-start.1 = (bf16[256,128]{1,0:T(8,128)(2,1)S(1)}, bf16[256,128]{1,0:T(8,128)(2,1)}, u32[]{:S(2)}) copy-start(bf16[256,128]{1,0:T(8,128)(2,1)} %constant.23.clone.of_ref) | copy-start | bytes 196612
  53.4 2.2 %copy-start.2 = (f32[128,128]{1,0:T(8,128)S(1)}, f32[128,128]{1,0:T(8,128)}, u32[]{:S(2)}) copy-start(f32[128,128]{1,0:T(8,128)} %constant.27.clone.tr_ref) | copy-start | bytes 196612
  53.4 2.2 %copy-start.3 = (f32[128,128]{1,0:T(8,128)S(1)}, f32[128,128]{1,0:T(8,128)}, u32[]{:S(2)}) copy-start(f32[128,128]{1,0:T(8,128)} %constant.28.clone.ti_ref) | copy-start | bytes 196612
  55.7 1.0 copy-start.6
  55.7 1.1 copy-start.9
  55.7 1.0 copy-start.12
  67.5 18.3 %all-to-all-start.1 = ((bf16[4,16,4096]{2,1,0:T(8,128)(2,1)}), bf16[4,16,4096]{2,1,0:T(8,128)(2,1)}, u32[]{:S(2)}, u32[]{:S(2)}) async-start(bf16[4,16,4096]{2,1,0:T(8,128)(2,1)} %copy-done.8), calls=%async_computation.1 | async-start | bytes 1048576 | tf_op jit(solution)/shard_map/all_to_all | solution.py:163
  71.7 1.0 copy-start.5
  71.7 1.1 copy-start.10
  85.8 18.3 %all-to-all-start.4 = ((bf16[4,16,4096]{2,1,0:T(8,128)(2,1)}), bf16[4,16,4096]{2,1,0:T(8,128)(2,1)}, u32[]{:S(2)}, u32[]{:S(2)}) async-start(bf16[4,16,4096]{2,1,0:T(8,128)(2,1)} %copy-done.7), calls=%async_computation.4 | async-start | bytes 1048576 | tf_op jit(solution)/shard_map/all_to_all | solution.py:163
  89.9 0.9 copy-start.11
  90.9 16.8 %copy-start.16 = (f32[192]{0:T(256)S(1)}, f32[192]{0:T(256)}, u32[]{:S(2)}) copy-start(f32[192]{0:T(256)} %param.16) | copy-start | bytes 2308
  90.9 30.6 %copy-start.14 = (bf16[192,4096]{1,0:T(8,128)(2,1)S(1)}, bf16[192,4096]{1,0:T(8,128)(2,1)}, u32[]{:S(2)}) copy-start(bf16[192,4096]{1,0:T(8,128)(2,1)} %param.13) | copy-start | bytes 4718596
  104.0 17.5 %all-to-all-start.7 = ((bf16[4,16,4096]{2,1,0:T(8,128)(2,1)}), bf16[4,16,4096]{2,1,0:T(8,128)(2,1)S(1)}, u32[]{:S(2)}, u32[]{:S(2)}) async-start(bf16[4,16,4096]{2,1,0:T(8,128)(2,1)} %long_conv.5), calls=%async_computation.7 | async-start | bytes 1048576 | tf_op jit(solution)/shard_map/all_to_all | solution.py:163
  126.0 13.4 %all-to-all-start.2 = ((bf16[8,64,512]{2,1,0:T(8,128)(2,1)}), bf16[8,64,512]{2,1,0:T(8,128)(2,1)S(1)}, u32[]{:S(2)}, u32[]{:S(2)}) async-start(bf16[8,64,512]{2,1,0:T(8,128)(2,1)} %bitcast.114), calls=%async_computation.2 | async-start | bytes 1048576 | tf_op jit(solution)/shard_map/all_to_all | solution.py:168
  139.4 13.1 %all-to-all-start.5 = ((bf16[8,64,512]{2,1,0:T(8,128)(2,1)}), bf16[8,64,512]{2,1,0:T(8,128)(2,1)S(1)}, u32[]{:S(2)}, u32[]{:S(2)}) async-start(bf16[8,64,512]{2,1,0:T(8,128)(2,1)} %bitcast.113), calls=%async_computation.5 | async-start | bytes 1048576 | tf_op jit(solution)/shard_map/all_to_all | solution.py:168
  152.5 5.2 %copy-start.15 = (bf16[8,64,512]{2,1,0:T(8,128)(2,1)}, bf16[8,64,512]{2,1,0:T(8,128)(2,1)S(1)}, u32[]{:S(2)}) copy-start(bf16[8,64,512]{2,1,0:T(8,128)(2,1)S(1)} %all-to-all-done.5) | copy-start | bytes 1572868
  152.5 13.9 %all-to-all-start.8 = ((bf16[8,64,512]{2,1,0:T(8,128)(2,1)}), bf16[8,64,512]{2,1,0:T(8,128)(2,1)}, u32[]{:S(2)}, u32[]{:S(2)}) async-start(bf16[8,64,512]{2,1,0:T(8,128)(2,1)} %bitcast.112), calls=%async_computation.8 | async-start | bytes 1048576 | tf_op jit(solution)/shard_map/all_to_all | solution.py:168
  156.7 1.4 copy-start.13
  (2 other events, 1.6 us)
Sparse Core Ops, SparseCore 0:
  9.2 41.4 all-gather.1
